TPU v7x, 128 devices: a whole 4x4x4 slice. The times are simulated.
128 devices in a mesh: group: 8 (over y_lo, z), shard: 16 (over y_hi, x, core).
Axes of the slice: x: 4, y: 4 (y_hi: 2, y_lo: 2; y = y_hi * 2 + y_lo), z: 4, core: 2. Of those that a mesh axis runs over, the one named last changes fastest.
Arguments:
- tokens: bfloat16 [196608, 1024], P(('group', 'shard')), may hold values from -36 to 36
- cotangent: bfloat16 [196608, 1024], P(('group', 'shard')), may hold values from -0.3046875 to 0.3046875
- master: float32 [8192, 4096], P(('group', 'shard')), may hold values from -0.03125 to 0.03125
- moment_one: float32 [8192, 4096], P(('group', 'shard')), may hold values from -2 to 2
- moment_two: float32 [8192, 4096], P(('group', 'shard')), may hold values from 0.05 to 2
- anchor: float32 [1024, 4096], P('shard'), may hold values from -0.03125 to 0.03125
- outer_momentum: float32 [1024, 4096], P('shard'), may hold values from -0.02 to 0.02
Outputs:
- moment_one_next: float32 [8192, 4096], P(('group', 'shard'))
- moment_two_next: float32 [8192, 4096], P(('group', 'shard'))
- momentum_next: float32 [1024, 4096], P('shard')
- anchor_next: float32 [1024, 4096], P('shard')
All inputs are finite; a program needn't handle non-finite values.
Results may differ from a plain program's by a relative error of at most 0.0047.
Values may be sent and summed in bfloat16 or wider, within the bound.
A program may use at most 128 MiB of HBM per device.

v0:
```python
import jax
import jax.numpy as jnp
from jax import lax
from jax.sharding import PartitionSpec as P

first_correction = 0.9999734386011124
second_correction = 0.994079470779664


def split_up(value, dim, count):
    dims = value.shape
    parts = value.reshape(*dims[:dim], count, dims[dim] // count, *dims[dim + 1 :])
    return jnp.moveaxis(parts, dim, 0)


def sent_and_summed(value, axis, dim):
    parts = split_up(value, dim, lax.axis_size(axis))
    arrived = lax.all_to_all(parts, axis, split_axis=0, concat_axis=0, tiled=True)
    return arrived.sum(axis=0)


def side_by_side(arrays, axis, dim, along):
    ends, at = ([], 0)
    for a in arrays[:-1]:
        at += a.shape[along]
        ends.append(at)
    both = jnp.concatenate(arrays, axis=along)
    return tuple(jnp.split(lax.all_gather(both, axis, axis=dim, tiled=True), ends, axis=along))


def gelu_tanh(values):
    return jax.nn.gelu(values, approximate=True)


def column_product(left, right):
    return lax.dot_general(
        left, right, (((0,), (0,)), ((), ())), preferred_element_type=jnp.float32
    )


def shards(tokens, cotangent, master, moment_one, moment_two, anchor, outer_momentum):
    working = master.astype(jnp.bfloat16)
    width = working.shape[1] // 2
    piece = lax.all_gather(working, "shard", axis=0, tiled=True)
    inputs = tokens
    upstream = cotangent
    pre_part = jnp.dot(inputs, piece[:, :width], preferred_element_type=jnp.float32)
    back_part = jnp.dot(upstream, piece[:, width:], preferred_element_type=jnp.float32)
    act = gelu_tanh(pre_part).astype(jnp.bfloat16)
    _, pullback = jax.vjp(gelu_tanh, pre_part)
    dpre = pullback(back_part)[0].astype(jnp.bfloat16)
    inputs = tokens
    upstream = cotangent
    grad = lax.psum_scatter(
        jnp.concatenate([column_product(inputs, dpre), column_product(upstream, act)], axis=1),
        "shard",
        scatter_dimension=0,
        tiled=True,
    )
    first = 0.9 * moment_one + 0.1 * grad
    second = 0.95 * moment_two + 0.05 * grad * grad
    update = first / first_correction / (jnp.sqrt(second / second_correction) + 1e-08)
    inner = master - 0.001 * (update + 0.1 * master)
    delta = anchor - inner
    groups = lax.axis_size("group")
    summed = sent_and_summed(delta, "group", 1)
    share = summed.shape[1]
    offset = lax.axis_index("group") * share
    momentum_share = lax.dynamic_slice_in_dim(outer_momentum, offset, share, 1)
    anchor_share = lax.dynamic_slice_in_dim(anchor, offset, share, 1)
    mean_delta = summed / groups
    momentum_part = 0.9 * momentum_share + mean_delta
    anchor_part = anchor_share - 0.7 * (mean_delta + 0.9 * momentum_part)
    momentum_next, anchor_next = side_by_side((momentum_part, anchor_part), "group", 1, 0)
    return (first, second, momentum_next, anchor_next)


def solution(mesh):
    placed = (
        P(("group", "shard"), None),
        P(("group", "shard"), None),
        P(("group", "shard"), None),
        P(("group", "shard"), None),
        P(("group", "shard"), None),
        P("shard", None),
        P("shard", None),
    )
    return jax.shard_map(
        shards,
        mesh=mesh,
        in_specs=placed,
        out_specs=(
            P(("group", "shard"), None),
            P(("group", "shard"), None),
            P("shard", None),
            P("shard", None),
        ),
        check_vma=False,
    )
```

profile of v0, /device:TPU:0, one launch (start us, length us, event | category | flops | bytes accessed | tf_op | source)
XLA Modules:
  0.0 394.4 jit_solution(9829937297733833045)
XLA Ops:
  7.2 0.0 copy-start
  7.2 0.0 all-gather.3.cloned.1.call-start
  7.2 2.2 convert_element_type.9
  9.5 0.0 all-gather.3.cloned.1.call-update
  9.5 0.0 reduce-scatter.4.cloned.1.call-start
  9.5 76.7 %all-gather.3.cloned.1.call-done = bf16[1024,4096]{1,0:T(8,128)(2,1)} async-done(((bf16[64,4096]{1,0:T(8,128)(2,1)}), bf16[1024,4096]{1,0:T(8,128)(2,1)}) %all-gather.3.cloned.1.call-update) | async-done | bytes 8388624 | tf_op jit(solution)/shard_map/all_gather | solution.py:44
  86.3 0.0 copy-done
  86.3 0.0 copy-start.2
  86.3 8.8 %fusion.14 = f32[1536,2048]{1,0:T(8,128)S(1)} fusion(bf16[1536,1024]{1,0:T(8,128)(2,1)S(1)} %copy-done, bf16[1024,4096]{1,0:T(8,128)(2,1)} %all-gather.3.cloned.1.call-done), kind=kOutput, calls=%fused_computation.15 | convolution fusion | flops 6442450944 | bytes 19922944 | tf_op jit(solution)/shard_map/dot_general | solution.py:47
  95.1 0.0 copy-start.3
  95.1 4.5 %copy-done.3 = f32[1536,2048]{1,0:T(8,128)} copy-done((f32[1536,2048]{1,0:T(8,128)}, f32[1536,2048]{1,0:T(8,128)S(1)}, u32[]{:S(2)}) %copy-start.3) | copy-done | bytes 12582936
  99.6 0.0 copy-done.2
  99.6 10.3 %fusion.13 = f32[1024,2048]{0,1:T(8,128)} fusion(bf16[1536,1024]{1,0:T(8,128)(2,1)S(1)} %copy-done.2, f32[1536,2048]{1,0:T(8,128)S(1)} %fusion.14), kind=kOutput, calls=%fused_computation.14 | convolution fusion | flops 6470762496 | bytes 24117248 | tf_op jit(solution)/shard_map/dot_general | solution.py:36
  110.0 25.1 %fusion.10 = f32[1024,2048]{0,1:T(8,128)} fusion(bf16[1536,1024]{1,0:T(8,128)(2,1)S(1)} %copy-done, f32[1536,2048]{1,0:T(8,128)} %copy-done.3, bf16[1536,1024]{1,0:T(8,128)(2,1)} %param.8, bf16[1024,4096]{1,0:T(8,128)(2,1)} %all-gather.3.cloned.1.call-done), kind=kOutput, calls=%fused_computation.13 | convolution fusion | flops 12947816448 | bytes 31457280 | tf_op jit(solution)/shard_map/dot_general | solution.py:36
  135.0 11.5 %pad_maximum_fusion = f32[1024,4096]{0,1:T(8,128)} fusion(f32[1024,2048]{0,1:T(8,128)} %fusion.13, f32[1024,2048]{0,1:T(8,128)} %fusion.10), kind=kLoop, calls=%fused_computation.2 | loop fusion | flops 4194304 | bytes 33554432 | tf_op jit(solution)/shard_map/concatenate | solution.py:55
  146.6 17.4 %copy.40 = f32[1024,4096]{1,0:T(8,128)} copy(f32[1024,4096]{0,1:T(8,128)} %pad_maximum_fusion) | data formatting | bytes 33554432
  164.0 0.0 reduce-scatter.4.cloned.1.call-update
  164.0 145.1 %reduce-scatter.4.cloned.1.call-done = f32[64,4096]{1,0:T(8,128)} async-done(((f32[1024,4096]{1,0:T(8,128)}), f32[64,4096]{1,0:T(8,128)}) %reduce-scatter.4.cloned.1.call-update) | async-done | bytes 1048592 | tf_op jit(solution)/shard_map/reduce_scatter | solution.py:54
  309.2 0.0 copy-start.1
  309.2 4.8 %subtract_subtract_fusion = (f32[64,4096]{1,0:T(8,128)S(1)}, f32[64,4096]{1,0:T(8,128)}, f32[64,4096]{1,0:T(8,128)}) fusion(f32[64,4096]{1,0:T(8,128)} %param.12, f32[64,4096]{1,0:T(8,128)} %param.9, f32[64,4096]{1,0:T(8,128)} %reduce-scatter.4.cloned.1.call-done, f32[64,4096]{1,0:T(8,128)} %param.11, f32[64,4096]{1,0:T(8,128)} %param.10), kind=kLoop, calls=%fused_computation.22 | loop fusion | flops 4194304 | bytes 8388608 | tf_op jit(solution)/shard_map/sub | solution.py:64
  313.9 1.1 copy.47
  315.0 4.4 %all-to-all-start = ((f32[8,64,512]{2,1,0:T(8,128)}), f32[8,64,512]{2,1,0:T(8,128)}, u32[]{:S(2)}, u32[]{:S(2)}) async-start(f32[8,64,512]{2,1,0:T(8,128)} %bitcast.16), calls=%async_computation | async-start | bytes 2097152 | tf_op jit(solution)/shard_map/all_to_all | solution.py:18
  319.4 0.0 all-gather.5.cloned.1.call-start
  319.5 1.6 constant_dynamic-slice_fusion
  321.1 1.0 copy.43
  322.2 0.8 copy.44
  323.0 10.6 %all-to-all-done = f32[8,64,512]{2,1,0:T(8,128)} async-done(((f32[8,64,512]{2,1,0:T(8,128)}), f32[8,64,512]{2,1,0:T(8,128)}, u32[]{:S(2)}, u32[]{:S(2)}) %all-to-all-start) | async-done | bytes 1048608 | tf_op jit(solution)/shard_map/all_to_all | solution.py:18
  333.6 1.3 reduce_sum.9
  334.9 0.8 copy.42
  335.8 1.1 multiply_add_fusion.1
  336.9 0.8 pad_maximum_fusion.1
  337.7 0.0 all-gather.5.cloned.1.call-update
  337.7 39.0 %all-gather.5.cloned.1.call-done = f32[128,4096]{0,1:T(8,128)} async-done(((f32[128,512]{0,1:T(8,128)}), f32[128,4096]{0,1:T(8,128)}) %all-gather.5.cloned.1.call-update) | async-done | bytes 2097168 | tf_op jit(solution)/shard_map/all_gather | solution.py:28
  376.7 4.9 %fusion.34 = (f32[64,4096]{0,1:T(8,128)}, f32[64,4096]{0,1:T(8,128)}) fusion(f32[128,4096]{0,1:T(8,128)} %all-gather.5.cloned.1.call-done), kind=kLoop, calls=%fused_computation.39 | loop fusion | bytes 4194304 | tf_op jit(solution)/shard_map/split | solution.py:28
  381.6 3.1 copy.38
  384.7 3.1 copy.39
  387.9 0.0 copy-done.1
Async XLA Ops:
  7.2 79.1 %copy-start = (bf16[1536,1024]{1,0:T(8,128)(2,1)S(1)}, bf16[1536,1024]{1,0:T(8,128)(2,1)}, u32[]{:S(2)}) copy-start(bf16[1536,1024]{1,0:T(8,128)(2,1)} %param.7) | copy-start | bytes 9437188
  7.2 79.1 %all-gather.3.cloned.1.call-start = ((), (), s32[]{:S(2)}) async-start(), calls=%async_computation.2 | async-start | bytes 8912896 | tf_op jit(solution)/shard_map/all_gather | solution.py:44
  9.5 299.7 %reduce-scatter.4.cloned.1.call-start = ((), (), s32[]{:S(2)}) async-start(), calls=%async_computation.4 | async-start | bytes 17825792 | tf_op jit(solution)/shard_map/reduce_scatter | solution.py:54
  86.3 13.4 %copy-start.2 = (bf16[1536,1024]{1,0:T(8,128)(2,1)S(1)}, bf16[1536,1024]{1,0:T(8,128)(2,1)}, u32[]{:S(2)}) copy-start(bf16[1536,1024]{1,0:T(8,128)(2,1)} %param.8) | copy-start | bytes 9437188
  95.1 4.5 %copy-start.3 = (f32[1536,2048]{1,0:T(8,128)}, f32[1536,2048]{1,0:T(8,128)S(1)}, u32[]{:S(2)}) copy-start(f32[1536,2048]{1,0:T(8,128)S(1)} %fusion.14) | copy-start | bytes 37748740
  309.2 78.7 %copy-start.1 = (bf16[1536,1024]{1,0:T(8,128)(2,1)S(1)}, bf16[1536,1024]{1,0:T(8,128)(2,1)}, u32[]{:S(2)}) copy-start(bf16[1536,1024]{1,0:T(8,128)(2,1)} %param.7) | copy-start | bytes 9437188
  315.0 18.6 %all-to-all-start = ((f32[8,64,512]{2,1,0:T(8,128)}), f32[8,64,512]{2,1,0:T(8,128)}, u32[]{:S(2)}, u32[]{:S(2)}) async-start(f32[8,64,512]{2,1,0:T(8,128)} %bitcast.16), calls=%async_computation | async-start | bytes 2097152 | tf_op jit(solution)/shard_map/all_to_all | solution.py:18
  319.4 57.3 %all-gather.5.cloned.1.call-start = ((), (), s32[]{:S(2)}) async-start(), calls=%async_computation.3 | async-start | bytes 2359296 | tf_op jit(solution)/shard_map/all_gather | solution.py:28
Sparse Core Ops, SparseCore 0:
  11.0 75.2 all-gather.2
  164.2 144.9 reduce-scatter.3
  337.9 38.7 all-gather.4
where the time goes:
time: 395 us; the launch traced here: 394 us
  waiting for transfers between devices  271 us (69%)
  matrix products  44.2 us (11%)
  local copies, waits for them, and re-layouts  38.6 us (10%)
  other arithmetic  21.8 us (6%)
  between operations  13.8 us (3%)
  starting transfers between devices  4.57 us (1%)
    reduce_scatter x1, waiting for transfers between devices, shards(): lax.psum_scatter(jnp.concatenate([column_product(inputs, dpre), column_pr...  145 us
    all_gather x1, waiting for transfers between devices, shards(): piece = lax.all_gather(working, 'shard', axis=0, tiled=True)  76.7 us
    all_gather x1, waiting for transfers between devices, side_by_side(): lax.all_gather(both, axis, axis=dim, tiled=True)  39 us
    dot_general x2, matrix products, column_product(): lax.dot_general(left, right, (((0,), (0,)), ((), ())), preferred_element_...  35.4 us
    unnamed x14, local copies, waits for them, and re-layouts  31 us
    concatenate x1, other arithmetic, shards(): jnp.concatenate([column_product(inputs, dpre), column_product(upstream, a...  11.5 us
    all_to_all x1, waiting for transfers between devices, sent_and_summed(): lax.all_to_all(parts, axis, split_axis=0, concat_axis=0, tiled=True)  10.6 us
    dot_general x1, matrix products, shards(): jnp.dot(inputs, piece[:, :width], preferred_element_type=jnp.float32)  8.83 us
  transfers between devices with their start and end apart: 4, of which 4 were waited for; matrix products, arithmetic and copies ran while one was open for 1% of the time, Pallas kernels for 0%

commit v1 on v0

v1 whole, which is shorter than its diff:
```python
import functools
import jax
import jax.numpy as jnp
from jax import lax
from jax.experimental import pallas as pl
from jax.experimental.pallas import tpu as pltpu
from jax.sharding import PartitionSpec as P

first_correction = 0.9999734386011124
second_correction = 0.994079470779664
MESH = pl.DeviceIdType.MESH
BF = jnp.bfloat16
F32 = jnp.float32
NJ = 4
HB = 256
BT = 512
ROOT = 0.7978845608028654


def gelu_pair(pre, back):
    square = pre * pre
    t = jnp.tanh(pre * (ROOT + (ROOT * 0.044715) * square))
    half = 0.5 + 0.5 * t
    slope = half + pre * (0.5 * ROOT + (1.5 * ROOT * 0.044715) * square) * (1.0 - t * t)
    return pre * half, back * slope


def kernel(
    tok, cot, mas, mo1, mo2, anc, omo,
    o1, o2, om, oa,
    T, C, W, WS, mst, b1, b2, ba, bo, act, dpre, gx, gp, sb, rb, ys, yr, dl, dr, mr,
    loc, tks, tkr, ays, ayr, a1s, a1r, a2s, a2r, rss, rsr, ycs, ycr, m1s, m1r, m2s, m2r, outs,
):
    me = lax.axis_index("group")
    s = lax.axis_index("shard")
    y, x, c = s // 8, (s // 2) % 4, s % 2
    n = lax.axis_size("group")
    td = tok.shape[0]

    def dev(yy, xx, cc):
        return (me, yy * 8 + xx * 2 + cc)

    right = dev(y, lax.rem(x + 1, 4), c)
    left = dev(y, lax.rem(x + 3, 4), c)
    across = (dev(1 - y, x, c), dev(1 - y, x, 1 - c), dev(y, x, 1 - c))

    def send(src, dst, ss, rs, to):
        return pltpu.make_async_remote_copy(
            src_ref=src, dst_ref=dst, send_sem=ss, recv_sem=rs, device_id=to, device_id_type=MESH
        )

    loads = [pltpu.make_async_copy(mas, mst, loc.at[0])]
    for i, (a, b) in enumerate(((mo1, b1), (mo2, b2), (anc, ba), (omo, bo))):
        loads.append(pltpu.make_async_copy(a, b, loc.at[3 + i]))
    loads[0].start()

    def blocks():
        for xx in range(4):
            for yy in range(2):
                yield slice((yy * 4 + xx) * 128, (yy * 4 + xx) * 128 + 128), slice(
                    xx * 256 + yy * 128, xx * 256 + yy * 128 + 128
                )

    for k, (a, b) in enumerate(((tok, T), (cot, C))):
        for cs, cd in blocks():
            pltpu.make_async_copy(a.at[:, cs], b.at[pl.ds(0, td), cd], loc.at[1 + k]).start()

    barrier = pltpu.get_barrier_semaphore()
    for to in (right, left) + across:
        pl.semaphore_signal(barrier, inc=1, device_id=to, device_id_type=MESH)
    for o in range(1, 8):
        pl.semaphore_signal(barrier, inc=1, device_id=(lax.rem(me + o, n), s), device_id_type=MESH)
    pl.semaphore_wait(barrier, 12)

    mine = pl.ds(pl.multiple_of(x * 256 + y * 128 + c * 64, 64), 64)

    def ag_y(j, i):
        src = (W.at[j, mine], WS.at[j], WS.at[j])[i]
        return send(src, W.at[j, mine], ays.at[j, i], ayr.at[j, i], across[i])

    loads[0].wait()

    def cast(j, _):
        for k in range(2):
            a = pl.ds(pl.multiple_of(k * 2048 + c * 1024 + j * HB, HB), HB)
            b = pl.ds(pl.multiple_of(k * 2048 + (1 - c) * 1024 + j * HB, HB), HB)
            W[j, mine, k * HB : (k + 1) * HB] = mst[:, a].astype(BF)
            WS[j, :, k * HB : (k + 1) * HB] = mst[:, b].astype(BF)
        for i in range(3):
            ag_y(j, i).start()
        return 0

    lax.fori_loop(0, NJ, cast, 0)
    for k, (a, b) in enumerate(((tok, T), (cot, C))):
        for cs, cd in blocks():
            send(a.at[:, cs], b.at[pl.ds(td, td), cd], tks.at[k], tkr.at[k], across[2]).start()
    for cp in loads[1:]:
        cp.start()

    def rows(xx, lo, count):
        return pl.ds(pl.multiple_of(lax.rem(xx, 4) * 256 + lo, 128), count)

    def ag_1(j, i):
        r = rows(x, 0, 256)
        return send(W.at[j, r], W.at[j, r], a1s.at[j, i], a1r.at[j, i], (right, left)[i])

    def ag_1_in(j, i):
        r = rows(x + (3, 1)[i], 0, 256)
        return send(W.at[j, r], W.at[j, r], a1s.at[j, i], a1r.at[j, i], (right, left)[i])

    def ag_2(j, i):
        r = rows(x + (3, 1)[i], (0, 128)[i], 128)
        return send(W.at[j, r], W.at[j, r], a2s.at[j, i], a2r.at[j, i], (right, left)[i])

    def ag_2_in(j, i):
        r = rows(x + 2, (0, 128)[i], 128)
        return send(W.at[j, r], W.at[j, r], a2s.at[j, i], a2r.at[j, i], (right, left)[i])

    def gather_one(j):
        for i in range(3):
            ag_y(j, i).wait_recv()
        for i in range(2):
            ag_1(j, i).start()

    def gather_two(j):
        for i in range(2):
            ag_1_in(j, i).wait_recv()
        for i in range(2):
            ag_2(j, i).start()

    def gather_end(j):
        for i in range(2):
            ag_2_in(j, i).wait_recv()

    def forward(i, _):
        r = pl.ds(pl.multiple_of(i * BT, BT), BT)
        j = _
        pre = jnp.dot(T[r, :], W[j, :, :HB], preferred_element_type=F32)
        back = jnp.dot(C[r, :], W[j, :, HB:], preferred_element_type=F32)
        a, d = gelu_pair(pre, back)
        act[r, :] = a.astype(BF)
        dpre[r, :] = d.astype(BF)
        return _

    def grads(dest):
        q = pl.ds(pl.multiple_of(lax.rem(dest, 4) * 256, 256), 256)
        dims = (((0,), (0,)), ((), ()))
        return (
            lax.dot_general(T[:, q], dpre[...], dims, preferred_element_type=F32),
            lax.dot_general(C[:, q], act[...], dims, preferred_element_type=F32),
        )

    def put(ref, pair, r):
        ref[:, :HB] = pair[0][r].astype(ref.dtype)
        ref[:, HB:] = pair[1][r].astype(ref.dtype)

    upper, lower = slice(0, 128), slice(128, 256)

    def rs(j, i):
        to = right if i in (0, 2, 4) else left
        return send(sb.at[j, i], rb.at[j, i], rss.at[j, i], rsr.at[j, i], to)

    def yc(j, i):
        return send(ys.at[j, i], yr.at[j, i], ycs.at[j, i], ycr.at[j, i], across[i])

    def reduce_one(j):
        for i in range(2):
            rs(j, i).wait_recv()
            sb[j, 4 + i] = (gp[j, i] + rb[j, i].astype(F32)).astype(BF)
            rs(j, 4 + i).start()

    def reduce_two(j):
        for i in (2, 3, 4, 5):
            rs(j, i).wait_recv()
        gx[j, upper] = gx[j, upper] + rb[j, 3].astype(F32) + rb[j, 4].astype(F32)
        gx[j, lower] = gx[j, lower] + rb[j, 2].astype(F32) + rb[j, 5].astype(F32)
        for i, (yy, cc) in enumerate(((1 - y, c), (1 - y, 1 - c), (y, 1 - c))):
            r = pl.ds(pl.multiple_of(yy * 128 + cc * 64, 64), 64)
            ys[j, i] = gx[j, r].astype(BF)
            yc(j, i).start()

    def out_copy(buf, ref, k, j, cols):
        return pltpu.make_async_copy(buf.at[:, cols], ref.at[:, cols], outs.at[k])

    def to_member(buf, slot, j, o, ss, rs_):
        i = lax.rem(me + o, n)
        return send(buf.at[j, slot(i)], (dr if buf is dl else mr).at[j, me], ss, rs_, (i, s))

    def step(j):
        for i in range(3):
            yc(j, i).wait_recv()
        r = pl.ds(pl.multiple_of(y * 128 + c * 64, 64), 64)
        sums = (
            (c, gx[j, r] + yr[j, 0].astype(F32)),
            (1 - c, yr[j, 1].astype(F32) + yr[j, 2].astype(F32)),
        )
        for h, total in sums:
            for k in range(2):
                cols = pl.ds(pl.multiple_of(k * 2048 + h * 1024 + j * HB, HB), HB)
                g = total[:, k * HB : (k + 1) * HB]
                first = 0.9 * b1[:, cols] + 0.1 * g
                second = 0.95 * b2[:, cols] + 0.05 * g * g
                update = first / first_correction / (jnp.sqrt(second / second_correction) + 1e-08)
                p = mst[:, cols]
                inner = p - 0.001 * (update + 0.1 * p)
                delta = ba[:, cols] - inner
                b1[:, cols] = first
                b2[:, cols] = second
                out_copy(b1, o1, 0, j, cols).start()
                out_copy(b2, o2, 1, j, cols).start()
                for t in range(2):
                    dl[j, 4 * h + 2 * k + t] = delta[:, t * 128 : (t + 1) * 128].astype(BF)
        for o in range(1, 8):
            to_member(dl, lambda i: i, j, o, m1s.at[j], m1r.at[j]).start()

    def bytes_of_seven(ref, j, sem):
        seven = ref.at[j, pl.ds(0, 7)]
        return pltpu.make_async_copy(seven, seven, sem)

    def mean(j):
        bytes_of_seven(dr, j, m1r.at[j]).wait()
        total = dl[j, me].astype(F32)
        for o in range(1, 8):
            total = total + dr[j, lax.rem(me + o, n)].astype(F32)
        mr[j, me] = total / n
        for o in range(1, 8):
            to_member(mr, lambda i: me, j, o, m2s.at[j], m2r.at[j]).start()

    def outer(j):
        bytes_of_seven(mr, j, m2r.at[j]).wait()
        for h in range(2):
            for k in range(2):
                for t in range(2):
                    cols = pl.ds(
                        pl.multiple_of(k * 2048 + h * 1024 + j * HB + t * 128, 128), 128
                    )
                    m = mr[j, 4 * h + 2 * k + t]
                    momentum = 0.9 * bo[:, cols] + m
                    bo[:, cols] = momentum
                    ba[:, cols] = ba[:, cols] - 0.7 * (m + 0.9 * momentum)
                cols = pl.ds(pl.multiple_of(k * 2048 + h * 1024 + j * HB, HB), HB)
                out_copy(bo, om, 2, j, cols).start()
                out_copy(ba, oa, 3, j, cols).start()

    gather_one(0)
    gather_one(1)
    gather_two(0)
    gather_one(2)
    half_t = pl.ds(0, td)
    late_t = pl.ds(td, td)
    for k, b in enumerate((T, C)):
        pltpu.make_async_copy(b.at[half_t], b.at[half_t], loc.at[1 + k]).wait()

    def chunk(j, _):
        gather_end(j)
        lax.fori_loop(0, td // BT, forward, j)

        @pl.when(j == 0)
        def _():
            for k, b in enumerate((T, C)):
                pltpu.make_async_copy(b.at[late_t], b.at[late_t], tkr.at[k]).wait()

        @pl.when(j >= 1)
        def _():
            reduce_one(j - 1)

        @pl.when(j < NJ - 1)
        def _():
            gather_two(j + 1)

        @pl.when(j == 0)
        def _():
            gather_one(3)

        lax.fori_loop(td // BT, 2 * td // BT, forward, j)

        @pl.when(j >= 2)
        def _():
            mean(j - 2)

        pair = grads(x + 2)
        put(sb.at[j, 0], pair, upper)
        put(sb.at[j, 1], pair, lower)
        rs(j, 0).start()
        rs(j, 1).start()

        @pl.when(j >= 1)
        def _():
            reduce_two(j - 1)

        pair = grads(x + 1)
        put(gp.at[j, 0], pair, upper)
        put(sb.at[j, 2], pair, lower)
        rs(j, 2).start()
        pair = grads(x + 3)
        put(gp.at[j, 1], pair, lower)
        put(sb.at[j, 3], pair, upper)
        rs(j, 3).start()
        pair = grads(x)
        put(gx.at[j], pair, slice(0, 256))

        @pl.when(j == 1)
        def _():
            for cp in loads[1:]:
                cp.wait()

        @pl.when(j >= 1)
        def _():
            step(j - 1)

        @pl.when(j >= 2)
        def _():
            outer(j - 2)

        return 0

    lax.fori_loop(0, NJ, chunk, 0)
    last = NJ - 1
    reduce_one(last)
    mean(last - 1)
    reduce_two(last)
    outer(last - 1)
    step(last)
    mean(last)
    outer(last)

    def drain(j, _):
        for i in range(3):
            ag_y(j, i).wait_send()
            yc(j, i).wait_send()
        for i in range(2):
            ag_1(j, i).wait_send()
            ag_2(j, i).wait_send()
        for i in range(6):
            rs(j, i).wait_send()
        bytes_of_seven(dl, j, m1s.at[j]).wait()
        bytes_of_seven(mr, j, m2s.at[j]).wait()
        return 0

    lax.fori_loop(0, NJ, drain, 0)
    for k, b in enumerate((T, C)):
        pltpu.make_async_copy(b.at[half_t], b.at[half_t], tks.at[k]).wait()
    for k, (buf, ref) in enumerate(((b1, o1), (b2, o2), (bo, om), (ba, oa))):
        pltpu.make_async_copy(buf, ref, outs.at[k]).wait()


def shards(tokens, cotangent, master, moment_one, moment_two, anchor, outer_momentum):
    td, d = tokens.shape
    r, w = master.shape
    vm = pltpu.VMEM
    dma = pltpu.SemaphoreType.DMA
    wide = jax.ShapeDtypeStruct((r, w), F32)
    any_ = pl.BlockSpec(memory_space=pl.ANY)
    return pl.pallas_call(
        kernel,
        out_shape=(wide,) * 4,
        in_specs=[any_] * 7,
        out_specs=(any_,) * 4,
        scratch_shapes=[
            vm((2 * td, d), BF), vm((2 * td, d), BF), vm((NJ, d, 2 * HB), BF), vm((NJ, r, 2 * HB), BF),
            vm((r, w), F32), vm((r, w), F32), vm((r, w), F32), vm((r, w), F32), vm((r, w), F32),
            vm((2 * td, HB), BF), vm((2 * td, HB), BF),
            vm((NJ, 256, 2 * HB), F32), vm((NJ, 2, 128, 2 * HB), F32),
            vm((NJ, 6, 128, 2 * HB), BF), vm((NJ, 6, 128, 2 * HB), BF),
            vm((NJ, 3, r, 2 * HB), BF), vm((NJ, 3, r, 2 * HB), BF),
            vm((NJ, 8, r, 128), BF), vm((NJ, 8, r, 128), BF), vm((NJ, 8, r, 128), F32),
            dma((7,)), dma((2,)), dma((2,)),
            dma((NJ, 3)), dma((NJ, 3)), dma((NJ, 2)), dma((NJ, 2)), dma((NJ, 2)), dma((NJ, 2)),
            dma((NJ, 6)), dma((NJ, 6)), dma((NJ, 3)), dma((NJ, 3)),
            dma((NJ,)), dma((NJ,)), dma((NJ,)), dma((NJ,)), dma((4,)),
        ],
        compiler_params=pltpu.CompilerParams(
            collective_id=0, has_side_effects=True, vmem_limit_bytes=62 * 1024 * 1024
        ),
        cost_estimate=pl.CostEstimate(
            flops=4 * 2 * td * d * 2048, bytes_accessed=16 << 20, transcendentals=0
        ),
        name="outer_step",
    )(tokens, cotangent, master, moment_one, moment_two, anchor, outer_momentum)


def solution(mesh):
    rows = P(("group", "shard"), None)
    own = P("shard", None)
    return jax.shard_map(
        shards,
        mesh=mesh,
        in_specs=(rows, rows, rows, rows, rows, own, own),
        out_specs=(rows, rows, own, own),
        check_vma=False,
    )
```

time: 395 us -> 116 us (0.29)
  waiting for transfers between devices: 271 us -> 0 us
  Pallas kernels: 0 us -> 109 us
  matrix products: 44.2 us -> 0 us
  local copies, waits for them, and re-layouts: 38.6 us -> 6.63 us
  other arithmetic: 21.8 us -> 0 us
  between operations: 13.8 us -> 0.66 us
  starting transfers between devices: 4.57 us -> 0 us
    reduce_scatter x1 -> x0, waiting for transfers between devices: 145 us -> none  [shards(): lax.psum_scatter(jnp.concatenate([column_product(inputs, dpre), column_pr...]
    all_gather x2 -> x0, waiting for transfers between devices: 116 us -> none  [the longest x1 76.7 us: shards(): piece = lax.all_gather(working, 'shard', axis=0, tiled=True)]
    pallas_call x0 -> x1, Pallas kernels: none -> 109 us  [shards(): pl.pallas_call(kernel, out_shape=(wide,) * 4, in_specs=[any_] * 7, out_sp...]
    dot_general x3 -> x0, matrix products: 44.2 us -> none  [the longest x2 35.4 us: column_product(): lax.dot_general(left, right, (((0,), (0,)), ((), ())), preferred_element_...]
    unnamed x14 -> x8, local copies, waits for them, and re-layouts: 31 us -> 6.63 us
    concatenate x2 -> x0, other arithmetic: 12.4 us -> none  [the longest x1 11.5 us: shards(): jnp.concatenate([column_product(inputs, dpre), column_product(upstream, a...]
    all_to_all x1 -> x0, waiting for transfers between devices: 10.6 us -> none  [sent_and_summed(): lax.all_to_all(parts, axis, split_axis=0, concat_axis=0, tiled=True)]
    split x1 -> x0, local copies, waits for them, and re-layouts: 4.87 us -> none  [side_by_side(): jnp.split(lax.all_gather(both, axis, axis=dim, tiled=True), ends, axis=al...]
  transfers between devices with their start and end apart: 4 -> 0, of which waited for: 4 -> 0; matrix products, arithmetic and copies ran while one was open for 1% -> 0% of each run, Pallas kernels for 0% -> 0%
where the time goes in v1:
time: 116 us
  Pallas kernels  109 us (94%)
  local copies, waits for them, and re-layouts  6.63 us (6%)
    pallas_call x1, Pallas kernels, shards(): pl.pallas_call(kernel, out_shape=(wide,) * 4, in_specs=[any_] * 7, out_sp...  109 us
    unnamed x8, local copies, waits for them, and re-layouts  6.63 us

profile of v1, /device:TPU:0, one launch (start us, length us, event | category | flops | bytes accessed | tf_op | source)
XLA Modules:
  0.0 116.1 jit_solution(9635018566882871950)
XLA Ops:
  0.6 108.8 %outer_step.1 = (f32[64,4096]{1,0:T(8,128)}, f32[64,4096]{1,0:T(8,128)}, f32[64,4096]{1,0:T(8,128)}, f32[64,4096]{1,0:T(8,128)}) custom-call(bf16[1536,1024]{1,0:T(8,128)(2,1)} %tok.1, bf16[1536,1024]{1,0:T(8,128)(2,1)} %cot.1, f32[64,4096]{1,0:T(8,128)} %mas.1, f32[64,4096]{1,0:T(8,128)} %mo1.1, f32[64,4096]{1,0:T(8,128)} %mo2.1, f32[64,4096]{1,0:T(8,128)} %anc.1, ...), custom_call_target="tpu_custom_call" | custom-call | flops 25769803776 | bytes 16777216 | tf_op jit(solution)/shard_map/outer_step/pallas_call | solution.py:354
  109.5 0.0 copy-start.1
  109.5 0.0 copy-start
  109.5 2.4 %copy.15 = f32[64,4096]{1,0:T(8,128)} copy(f32[64,4096]{1,0:T(8,128)} %get-tuple-element.8) | data formatting | bytes 2097152
  111.9 2.3 %copy.16 = f32[64,4096]{1,0:T(8,128)} copy(f32[64,4096]{1,0:T(8,128)} %get-tuple-element.9) | data formatting | bytes 2097152
  114.2 0.0 copy-done.1
  114.2 1.0 copy.17
  115.1 0.0 copy-done
  115.2 1.0 copy.18
Async XLA Ops:
  109.5 4.7 %copy-start.1 = (f32[64,4096]{1,0:T(8,128)S(1)}, f32[64,4096]{1,0:T(8,128)}, u32[]{:S(2)}) copy-start(f32[64,4096]{1,0:T(8,128)} %get-tuple-element.10) | copy-start | bytes 3145732
  109.5 5.7 %copy-start = (f32[64,4096]{1,0:T(8,128)S(1)}, f32[64,4096]{1,0:T(8,128)}, u32[]{:S(2)}) copy-start(f32[64,4096]{1,0:T(8,128)} %get-tuple-element.11) | copy-start | bytes 3145732

commit v2 on v0

v2 whole, which is shorter than its diff:
```python
import functools
import jax
import jax.numpy as jnp
from jax import lax
from jax.experimental import pallas as pl
from jax.experimental.pallas import tpu as pltpu
from jax.sharding import PartitionSpec as P

first_correction = 0.9999734386011124
second_correction = 0.994079470779664
MESH = pl.DeviceIdType.MESH
BF = jnp.bfloat16
F32 = jnp.float32
NJ = 4
NU = 2 * NJ
HB = 256
VMEM_MIB = 49
BT = 512
ROOT = 0.7978845608028654


def gelu_pair(pre, back):
    square = pre * pre
    t = jnp.tanh(pre * (ROOT + (ROOT * 0.044715) * square))
    half = 0.5 + 0.5 * t
    slope = half + pre * (0.5 * ROOT + (1.5 * ROOT * 0.044715) * square) * (1.0 - t * t)
    return pre * half, back * slope


def kernel(
    tok, cot, mas, mo1, mo2, anc, omo,
    o1, o2, om, oa,
    T, C, W, WS, mst, b1, b2, ba, bo, act, dpre, pool, sb, rb, ys, yr, dl, dr, mr,
    loc, tks, tkr, s1s, s1r, s2s, s2r, rss, rsr, ycs, ycr, m1s, m1r, m2s, m2r, outs,
):
    me = lax.axis_index("group")
    s = lax.axis_index("shard")
    y, x, c = s // 8, (s // 2) % 4, s % 2
    n = lax.axis_size("group")
    td = tok.shape[0]

    def dev(yy, xx, cc):
        return (me, yy * 8 + lax.rem(xx, 4) * 2 + cc)

    right, left = dev(y, x + 1, c), dev(y, x + 3, c)
    across = (dev(1 - y, x, c), dev(1 - y, x, 1 - c), dev(y, x, 1 - c))
    greeted = (right, left) + across + (dev(y, x + 1, 1 - c), dev(y, x + 3, 1 - c))
    first_to = across + (right, left) + greeted[5:]

    def send(src, dst, ss, rs, to):
        return pltpu.make_async_remote_copy(
            src_ref=src, dst_ref=dst, send_sem=ss, recv_sem=rs, device_id=to, device_id_type=MESH
        )

    loads = [pltpu.make_async_copy(mas, mst, loc.at[0])]
    for i, (a, b) in enumerate(((mo1, b1), (mo2, b2), (anc, ba), (omo, bo))):
        loads.append(pltpu.make_async_copy(a, b, loc.at[3 + i]))
    loads[0].start()

    def blocks():
        for k in range(4):
            for yy in range(2):
                at = (yy * 4 + lax.rem(x + k, 4)) * 128
                yield pl.ds(pl.multiple_of(at, 128), 128), slice(k * 256 + yy * 128, k * 256 + yy * 128 + 128)

    for k, (a, b) in enumerate(((tok, T), (cot, C))):
        for cs, cd in blocks():
            pltpu.make_async_copy(a.at[:, cs], b.at[pl.ds(0, td), cd], loc.at[1 + k]).start()

    barrier = pltpu.get_barrier_semaphore()
    for o in range(1, 8):
        pl.semaphore_signal(barrier, inc=1, device_id=(lax.rem(me + o, n), s), device_id_type=MESH)
    for to in greeted:
        pl.semaphore_signal(barrier, inc=1, device_id=to, device_id_type=MESH)

    def rows(k, yy, cc=0, count=64):
        return pl.ds(pl.multiple_of((k % 4) * 256 + yy * 128 + cc * 64, 64), count)

    mine = rows(0, y, c)

    def weight(j, k, sems, src, dst, to):
        ss, rs_ = sems
        return send(src, W.at[j, dst], ss.at[j, k], rs_.at[j, k], to)

    def g1(j, k):
        src = W.at[j, mine] if k in (0, 3, 4) else WS.at[j]
        dst = rows((0, 0, 0, 3, 1, 3, 1)[k], y, c)
        return weight(j, k, (s1s, s1r), src, dst, first_to[k])

    def g2(j, k):
        a, b, yy, cc, count = (
            (0, 3, 1 - y, 0, 128), (0, 1, 1 - y, 0, 128),
            (3, 2, y, 0, 64), (1, 2, y, 1, 64),
            (3, 2, 1 - y, 0, 64), (1, 2, 1 - y, 1, 64),
            (2, 2, y, 0, 128), (3, 3, y, 0, 128), (1, 1, y, 0, 128),
        )[k]
        to = across[0] if k >= 6 else (right, left)[k % 2]
        return weight(j, k, (s2s, s2r), W.at[j, rows(a, yy, cc, count)], rows(b, yy, cc, count), to)

    def arrive(f, j, *ks):
        for k in ks:
            f(j, k).wait_recv()

    def go(f, j, *ks):
        for k in ks:
            f(j, k).start()

    def near_y(j):
        go(g1, j, 0, 1, 2)

    def near_x(j):
        go(g1, j, 3, 4, 5, 6)

    def pass_own(j):
        arrive(g1, j, 3, 5)
        go(g2, j, 2)
        arrive(g1, j, 4, 6)
        go(g2, j, 3)
        if j > 0:
            go(g2, j, 7, 8)

    def pass_other(j):
        arrive(g1, j, 0, 1)
        go(g2, j, 0, 1)

    def pass_far(j):
        if j == 0:
            arrive(g2, j, 0)
            go(g2, j, 4)
            arrive(g2, j, 1)
            go(g2, j, 5)
        else:
            arrive(g2, j, 2, 3)
            go(g2, j, 6)

    def gather_end(j):
        if j == 0:
            arrive(g2, j, 2, 3, 4, 5)
        else:
            arrive(g1, j, 0, 1, 2)
            arrive(g2, j, 7, 8, 6)

    loads[0].wait()

    def cast(j, _):
        for k in range(2):
            a = pl.ds(pl.multiple_of(k * 2048 + c * 1024 + j * HB, HB), HB)
            b = pl.ds(pl.multiple_of(k * 2048 + (1 - c) * 1024 + j * HB, HB), HB)
            W[j, mine, k * HB : (k + 1) * HB] = mst[:, a].astype(BF)
            WS[j, :, k * HB : (k + 1) * HB] = mst[:, b].astype(BF)
        return 0

    lax.fori_loop(0, NJ, cast, 0)
    pl.semaphore_wait(barrier, 14)

    near_y(0)
    near_x(0)
    near_y(1)
    near_x(1)
    near_y(2)
    near_y(3)
    for k, (a, b) in enumerate(((tok, T), (cot, C))):
        for cs, cd in blocks():
            send(a.at[:, cs], b.at[pl.ds(td, td), cd], tks.at[k], tkr.at[k], across[2]).start()
    for cp in loads[1:]:
        cp.start()

    def tile(i):
        return pl.ds(pl.multiple_of(i * BT, BT), BT)

    def finish(r, pre, back):
        a, d = gelu_pair(pre, back)
        act[r, :] = a.astype(BF)
        dpre[r, :] = d.astype(BF)

    def forward(i, j):
        r = slice(i * td, (i + 1) * td)
        pre = jnp.dot(T[r, :], W[j, :, :HB], preferred_element_type=F32)
        back = jnp.dot(C[r, :], W[j, :, HB:], preferred_element_type=F32)
        finish(r, pre, back)

    def product(r, k):
        q = slice(k * 256, k * 256 + 256)
        return (
            jnp.dot(T[r, q], W[0, q, :HB], preferred_element_type=F32),
            jnp.dot(C[r, q], W[0, q, HB:], preferred_element_type=F32),
        )

    def part(i, k):
        return pl.ds(pl.multiple_of(k * 2 * td + i * BT, BT), BT)

    def early(i, _):
        r = tile(i)
        a, b, d = product(r, 0), product(r, 1), product(r, 3)
        for k in range(2):
            pool[part(i, k), :] = a[k] + b[k] + d[k]
        return 0

    def late(i, _):
        r = tile(i)
        a = product(r, 2)
        finish(r, pool[part(i, 0), :] + a[0], pool[part(i, 1), :] + a[1])
        return 0

    half = td // BT
    half_t = pl.ds(0, td)
    late_t = pl.ds(td, td)

    def tokens_own():
        arrive(g1, 0, 2)
        for k, b in enumerate((T, C)):
            pltpu.make_async_copy(b.at[half_t], b.at[half_t], loc.at[1 + k]).wait()

    def tokens_other():
        for k, b in enumerate((T, C)):
            pltpu.make_async_copy(b.at[late_t], b.at[late_t], tkr.at[k]).wait()

    upper, lower = slice(0, 128), slice(128, 256)

    def rs(u, i):
        to = right if i in (0, 2, 4) else left
        return send(sb.at[u, i], rb.at[u, i], rss.at[u, i], rsr.at[u, i], to)

    def yc(u, i):
        return send(ys.at[u, i], yr.at[u, i], ycs.at[u, i], ycr.at[u, i], across[i])

    def gx(u):
        return pool.at[u * 256 : (u + 1) * 256]

    def gp(u, i):
        at = NU * 256 + u * 256 + i * 128
        return pool.at[at : at + 128]

    def grad(u):
        a, b = ((T, dpre), (C, act))[u % 2]
        dims = (((0,), (0,)), ((), ()))
        far = lax.dot_general(a[:, 512:], b[...], dims, preferred_element_type=F32)
        near = lax.dot_general(a[:, :512], b[...], dims, preferred_element_type=F32)
        for i, v in enumerate((far[:128], far[128:256], near[384:], far[256:384])):
            sb[u, i] = v.astype(BF)
        gx(u)[...] = near[:256]
        gp(u, 0)[...] = near[256:384]
        gp(u, 1)[...] = far[384:]
        for i in range(4):
            rs(u, i).start()

    def reduce_one(u):
        for i in range(2):
            rs(u, i).wait_recv()
            sb[u, 4 + i] = (gp(u, i)[...] + rb[u, i].astype(F32)).astype(BF)
            rs(u, 4 + i).start()

    def reduce_two(u):
        for i in (2, 3, 4, 5):
            rs(u, i).wait_recv()
        for r, a, b in ((upper, 3, 4), (lower, 2, 5)):
            gx(u)[r] = gx(u)[r] + rb[u, a].astype(F32) + rb[u, b].astype(F32)
        for i, (yy, cc) in enumerate(((1 - y, c), (1 - y, 1 - c), (y, 1 - c))):
            r = pl.ds(pl.multiple_of(yy * 128 + cc * 64, 64), 64)
            ys[u, i] = gx(u)[r].astype(BF)
            yc(u, i).start()

    def out_copy(buf, ref, k, cols):
        return pltpu.make_async_copy(buf.at[:, cols], ref.at[:, cols], outs.at[k])

    def columns(u, h):
        j, k = u // 2, u % 2
        return pl.ds(pl.multiple_of(k * 2048 + h * 1024 + j * HB, HB), HB)

    def eight(i):
        return pl.ds(pl.multiple_of(i * 8, 8), 8)

    def send_delta(u, o):
        i = lax.rem(me + o, n)
        return send(dl.at[u, eight(i)], dr.at[u, eight(me)], m1s.at[u], m1r.at[u], (i, s))

    def send_mean(u, o):
        i = lax.rem(me + o, n)
        return send(mr.at[u, eight(me)], mr.at[u, eight(me)], m2s.at[u], m2r.at[u], (i, s))

    def step(u):
        for i in range(3):
            yc(u, i).wait_recv()
        r = pl.ds(pl.multiple_of(y * 128 + c * 64, 64), 64)
        sums = (
            (c, gx(u)[r] + yr[u, 0].astype(F32)),
            (1 - c, yr[u, 1].astype(F32) + yr[u, 2].astype(F32)),
        )
        for h, g in sums:
            cols = columns(u, h)
            first = 0.9 * b1[:, cols] + 0.1 * g
            second = 0.95 * b2[:, cols] + 0.05 * g * g
            root = jnp.sqrt(second * (1.0 / second_correction)) + 1e-08
            update = first * (1.0 / first_correction) / root
            p = mst[:, cols]
            inner = p - 0.001 * (update + 0.1 * p)
            b1[:, cols] = first
            b2[:, cols] = second
            out_copy(b1, o1, 0, cols).start()
            out_copy(b2, o2, 1, cols).start()
            dl[u, :, pl.ds(pl.multiple_of(h * HB, HB), HB)] = ba[:, cols] - inner
        for o in range(1, 8):
            send_delta(u, o).start()

    def seven(ref, u, sem):
        part_ = ref.at[u, pl.ds(0, 56)]
        return pltpu.make_async_copy(part_, part_, sem)

    def mean(u):
        seven(dr, u, m1r.at[u]).wait()
        total = dl[u, eight(me)]
        for o in range(1, 8):
            total = total + dr[u, eight(lax.rem(me + o, n))]
        mr[u, eight(me)] = total / n
        for o in range(1, 8):
            send_mean(u, o).start()

    def outer(u):
        seven(mr, u, m2r.at[u]).wait()
        for h in range(2):
            cols = columns(u, h)
            m = mr[u, :, h * HB : (h + 1) * HB]
            momentum = 0.9 * bo[:, cols] + m
            bo[:, cols] = momentum
            ba[:, cols] = ba[:, cols] - 0.7 * (m + 0.9 * momentum)
            out_copy(bo, om, 2, cols).start()
            out_copy(ba, oa, 3, cols).start()

    pass_other(0)
    pass_own(0)
    pass_own(1)
    pass_far(0)
    near_x(2)
    tokens_own()
    lax.fori_loop(0, half, early, 0)
    tokens_other()
    lax.fori_loop(half, 2 * half, early, 0)
    pass_far(1)
    near_x(3)
    gather_end(0)
    lax.fori_loop(0, 2 * half, late, 0)
    pass_own(2)

    def both(f, j):
        if 0 <= j < NJ:
            f(2 * j + 1)
            f(2 * j)

    for j in range(NJ):
        if j > 0:
            gather_end(j)
            forward(0, j)
            if j == 2:
                for cp in loads[1:]:
                    cp.wait()
            both(reduce_two, j - 2)
            forward(1, j)
            if j == 1:
                pass_far(3)
            both(reduce_one, j - 1)
            both(mean, j - 3)
        grad(2 * j + 1)
        if j == 0:
            pass_own(3)
        grad(2 * j)
        if j == 0:
            pass_far(2)
        both(step, j - 2)
        both(outer, j - 3)

    p, q = NU - 2, NU - 1
    both(reduce_two, NJ - 2)
    reduce_one(q)
    reduce_one(p)
    both(mean, NJ - 3)
    both(step, NJ - 2)
    reduce_two(q)
    reduce_two(p)
    both(outer, NJ - 3)
    both(mean, NJ - 2)
    step(q)
    step(p)
    both(outer, NJ - 2)
    mean(q)
    mean(p)
    outer(q)
    outer(p)

    def drain(j, _):
        for k in range(7):
            g1(j, k).wait_send()
        for k in (2, 3):
            g2(j, k).wait_send()
        return 0

    def drain_sums(u, _):
        for i in range(3):
            yc(u, i).wait_send()
        for i in range(6):
            rs(u, i).wait_send()
        seven(dl, u, m1s.at[u]).wait()
        seven(mr, u, m2s.at[u]).wait()
        return 0

    lax.fori_loop(0, NJ, drain, 0)
    for j in range(NJ):
        for k in (6, 7, 8) if j else (0, 1, 4, 5):
            g2(j, k).wait_send()
    lax.fori_loop(0, NU, drain_sums, 0)
    for k, b in enumerate((T, C)):
        pltpu.make_async_copy(b.at[half_t], b.at[half_t], tks.at[k]).wait()
    for k, (buf, ref) in enumerate(((b1, o1), (b2, o2), (bo, om), (ba, oa))):
        pltpu.make_async_copy(buf, ref, outs.at[k]).wait()


def shards(tokens, cotangent, master, moment_one, moment_two, anchor, outer_momentum):
    td, d = tokens.shape
    r, w = master.shape
    vm = pltpu.VMEM
    dma = pltpu.SemaphoreType.DMA
    wide = jax.ShapeDtypeStruct((r, w), F32)
    return pl.pallas_call(
        kernel,
        out_shape=(wide,) * 4,
        in_specs=[pl.BlockSpec(memory_space=pltpu.HBM)] * 7,
        out_specs=(pl.BlockSpec(memory_space=pl.ANY),) * 4,
        scratch_shapes=[
            vm((2 * td, d), BF), vm((2 * td, d), BF), vm((NJ, d, 2 * HB), BF), vm((NJ, r, 2 * HB), BF),
            vm((r, w), F32), vm((r, w), F32), vm((r, w), F32), vm((r, w), F32), vm((r, w), F32),
            vm((2 * td, HB), BF), vm((2 * td, HB), BF), vm((4 * td, HB), F32),
            vm((NU, 6, 128, HB), BF), vm((NU, 6, 128, HB), BF),
            vm((NU, 3, r, HB), BF), vm((NU, 3, r, HB), BF),
            vm((NU, r, 2 * HB), F32), vm((NU, r, 2 * HB), F32), vm((NU, r, 2 * HB), F32),
            dma((7,)), dma((2,)), dma((2,)),
            dma((NJ, 7)), dma((NJ, 7)), dma((NJ, 9)), dma((NJ, 9)),
            dma((NU, 6)), dma((NU, 6)), dma((NU, 3)), dma((NU, 3)),
            dma((NU,)), dma((NU,)), dma((NU,)), dma((NU,)), dma((4,)),
        ],
        compiler_params=pltpu.CompilerParams(
            collective_id=0, has_side_effects=True, vmem_limit_bytes=VMEM_MIB * 1024 * 1024
        ),
        cost_estimate=pl.CostEstimate(
            flops=4 * 2 * td * d * 2048, bytes_accessed=16 << 20, transcendentals=0
        ),
        name="outer_step",
    )(tokens, cotangent, master, moment_one, moment_two, anchor, outer_momentum)


def solution(mesh):
    rows = P(("group", "shard"), None)
    own = P("shard", None)
    return jax.shard_map(
        shards,
        mesh=mesh,
        in_specs=(rows, rows, rows, rows, rows, own, own),
        out_specs=(rows, rows, own, own),
        check_vma=False,
    )
```

time: 395 us -> 97 us (0.25)
  waiting for transfers between devices: 271 us -> 0 us
  Pallas kernels: 0 us -> 92.4 us
  matrix products: 44.2 us -> 0 us
  local copies, waits for them, and re-layouts: 38.6 us -> 3.88 us
  other arithmetic: 21.8 us -> 0 us
  between operations: 13.8 us -> 0.64 us
  starting transfers between devices: 4.57 us -> 0 us
    reduce_scatter x1 -> x0, waiting for transfers between devices: 145 us -> none  [shards(): lax.psum_scatter(jnp.concatenate([column_product(inputs, dpre), column_pr...]
    all_gather x2 -> x0, waiting for transfers between devices: 116 us -> none  [the longest x1 76.7 us: shards(): piece = lax.all_gather(working, 'shard', axis=0, tiled=True)]
    pallas_call x0 -> x1, Pallas kernels: none -> 92.4 us  [shards(): pl.pallas_call(kernel, out_shape=(wide,) * 4, in_specs=[pl.BlockSpec(memo...]
    dot_general x3 -> x0, matrix products: 44.2 us -> none  [the longest x2 35.4 us: column_product(): lax.dot_general(left, right, (((0,), (0,)), ((), ())), preferred_element_...]
    unnamed x14 -> x4, local copies, waits for them, and re-layouts: 31 us -> 3.88 us
    concatenate x2 -> x0, other arithmetic: 12.4 us -> none  [the longest x1 11.5 us: shards(): jnp.concatenate([column_product(inputs, dpre), column_product(upstream, a...]
    all_to_all x1 -> x0, waiting for transfers between devices: 10.6 us -> none  [sent_and_summed(): lax.all_to_all(parts, axis, split_axis=0, concat_axis=0, tiled=True)]
    split x1 -> x0, local copies, waits for them, and re-layouts: 4.87 us -> none  [side_by_side(): jnp.split(lax.all_gather(both, axis, axis=dim, tiled=True), ends, axis=al...]
  transfers between devices with their start and end apart: 4 -> 0, of which waited for: 4 -> 0; matrix products, arithmetic and copies ran while one was open for 1% -> 0% of each run, Pallas kernels for 0% -> 0%
where the time goes in v2:
time: 97 us; the launch traced here: 96.9 us
  Pallas kernels  92.4 us (95%)
  local copies, waits for them, and re-layouts  3.88 us (4%)
    pallas_call x1, Pallas kernels, shards(): pl.pallas_call(kernel, out_shape=(wide,) * 4, in_specs=[pl.BlockSpec(memo...  92.4 us
    unnamed x4, local copies, waits for them, and re-layouts  3.88 us

profile of v2, /device:TPU:0, one launch (start us, length us, event | category | flops | bytes accessed | tf_op | source)
XLA Modules:
  0.0 96.9 jit_solution(8277244757216233223)
XLA Ops:
  0.6 92.4 %outer_step.1 = (f32[64,4096]{1,0:T(8,128)S(1)}, f32[64,4096]{1,0:T(8,128)S(1)}, f32[64,4096]{1,0:T(8,128)S(1)}, f32[64,4096]{1,0:T(8,128)S(1)}) custom-call(bf16[1536,1024]{1,0:T(8,128)(2,1)} %tok.1, bf16[1536,1024]{1,0:T(8,128)(2,1)} %cot.1, f32[64,4096]{1,0:T(8,128)} %mas.1, f32[64,4096]{1,0:T(8,128)} %mo1.1, f32[64,4096]{1,0:T(8,128)} %mo2.1, ...), custom_call_target="tpu_custom_call" | custom-call | flops 25769803776 | bytes 16777216 | tf_op jit(solution)/shard_map/outer_step/pallas_call | solution.py:422
  93.0 1.0 %copy.15 = f32[64,4096]{1,0:T(8,128)} copy(f32[64,4096]{1,0:T(8,128)S(1)} %get-tuple-element.8) | data formatting | bytes 2097152
  94.0 1.0 %copy.16 = f32[64,4096]{1,0:T(8,128)} copy(f32[64,4096]{1,0:T(8,128)S(1)} %get-tuple-element.9) | data formatting | bytes 2097152
  95.0 1.0 %copy.17 = f32[64,4096]{1,0:T(8,128)} copy(f32[64,4096]{1,0:T(8,128)S(1)} %get-tuple-element.10) | data formatting | bytes 2097152
  95.9 1.0 %copy.18 = f32[64,4096]{1,0:T(8,128)} copy(f32[64,4096]{1,0:T(8,128)S(1)} %get-tuple-element.11) | data formatting | bytes 2097152

commit v3 on v2

--- a/solution.py
+++ b/solution.py
@@ -19,18 +19,18 @@
 ROOT = 0.7978845608028654
 
 
-def gelu_pair(pre, back):
+def gelu_pair(pre):
     square = pre * pre
     t = jnp.tanh(pre * (ROOT + (ROOT * 0.044715) * square))
     half = 0.5 + 0.5 * t
     slope = half + pre * (0.5 * ROOT + (1.5 * ROOT * 0.044715) * square) * (1.0 - t * t)
-    return pre * half, back * slope
+    return pre * half, slope
 
 
 def kernel(
     tok, cot, mas, mo1, mo2, anc, omo,
     o1, o2, om, oa,
-    T, C, W, WS, mst, b1, b2, ba, bo, act, dpre, pool, sb, rb, ys, yr, dl, dr, mr,
+    T, C, W, WS, mst, b1, b2, ba, bo, act, dpre, slope, pool, sb, rb, ys, yr, dl, dr, mr,
     loc, tks, tkr, s1s, s1r, s2s, s2r, rss, rsr, ycs, ycr, m1s, m1r, m2s, m2r, outs,
 ):
     me = lax.axis_index("group")
@@ -80,12 +80,12 @@
 
     def weight(j, k, sems, src, dst, to):
         ss, rs_ = sems
-        return send(src, W.at[j, dst], ss.at[j, k], rs_.at[j, k], to)
+        return send(src, W.at[j, dst], ss.at[0], rs_.at[j, k], to)
 
     def g1(j, k):
         src = W.at[j, mine] if k in (0, 3, 4) else WS.at[j]
         dst = rows((0, 0, 0, 3, 1, 3, 1)[k], y, c)
-        return weight(j, k, (s1s, s1r), src, dst, first_to[k])
+        return weight(j, (0, 0, 0, 1, 2, 1, 2)[k], (s1s, s1r), src, dst, first_to[k])
 
     def g2(j, k):
         a, b, yy, cc, count = (
@@ -95,11 +95,12 @@
             (2, 2, y, 0, 128), (3, 3, y, 0, 128), (1, 1, y, 0, 128),
         )[k]
         to = across[0] if k >= 6 else (right, left)[k % 2]
-        return weight(j, k, (s2s, s2r), W.at[j, rows(a, yy, cc, count)], rows(b, yy, cc, count), to)
-
-    def arrive(f, j, *ks):
-        for k in ks:
-            f(j, k).wait_recv()
+        i = (0, 1, 2, 2, 2, 2)[k] if j == 0 else (0, 0, 0, 0, 0, 0, 1, 1, 1)[k]
+        return weight(j, i, (s2s, s2r), W.at[j, rows(a, yy, cc, count)], rows(b, yy, cc, count), to)
+
+    def arrive(sem, count):
+        some = W.at[0, pl.ds(0, count)]
+        pltpu.make_async_copy(some, some, sem).wait()
 
     def go(f, j, *ks):
         for k in ks:
@@ -112,33 +113,34 @@
         go(g1, j, 3, 4, 5, 6)
 
     def pass_own(j):
-        arrive(g1, j, 3, 5)
+        arrive(s1r.at[j, 1], 128)
         go(g2, j, 2)
-        arrive(g1, j, 4, 6)
+        arrive(s1r.at[j, 2], 128)
         go(g2, j, 3)
-        if j > 0:
-            go(g2, j, 7, 8)
+
+    def pass_along_y(j):
+        go(g2, j, 7, 8)
 
     def pass_other(j):
-        arrive(g1, j, 0, 1)
+        arrive(s1r.at[j, 0], 192)
         go(g2, j, 0, 1)
 
     def pass_far(j):
         if j == 0:
-            arrive(g2, j, 0)
+            arrive(s2r.at[j, 0], 128)
             go(g2, j, 4)
-            arrive(g2, j, 1)
+            arrive(s2r.at[j, 1], 128)
             go(g2, j, 5)
         else:
-            arrive(g2, j, 2, 3)
+            arrive(s2r.at[j, 0], 128)
             go(g2, j, 6)
 
     def gather_end(j):
         if j == 0:
-            arrive(g2, j, 2, 3, 4, 5)
+            arrive(s2r.at[j, 2], 256)
         else:
-            arrive(g1, j, 0, 1, 2)
-            arrive(g2, j, 7, 8, 6)
+            arrive(s1r.at[j, 0], 192)
+            arrive(s2r.at[j, 1], 384)
 
     loads[0].wait()
 
@@ -157,8 +159,6 @@
     near_x(0)
     near_y(1)
     near_x(1)
-    near_y(2)
-    near_y(3)
     for k, (a, b) in enumerate(((tok, T), (cot, C))):
         for cs, cd in blocks():
             send(a.at[:, cs], b.at[pl.ds(td, td), cd], tks.at[k], tkr.at[k], across[2]).start()
@@ -169,15 +169,29 @@
         return pl.ds(pl.multiple_of(i * BT, BT), BT)
 
     def finish(r, pre, back):
-        a, d = gelu_pair(pre, back)
+        a, d = gelu_pair(pre)
         act[r, :] = a.astype(BF)
-        dpre[r, :] = d.astype(BF)
+        dpre[r, :] = (back * d).astype(BF)
 
     def forward(i, j):
         r = slice(i * td, (i + 1) * td)
         pre = jnp.dot(T[r, :], W[j, :, :HB], preferred_element_type=F32)
         back = jnp.dot(C[r, :], W[j, :, HB:], preferred_element_type=F32)
         finish(r, pre, back)
+
+    halves = (slice(0, td), slice(td, 2 * td))
+
+    def forward_in(j):
+        pre = [jnp.dot(T[r, :], W[j, :, :HB], preferred_element_type=F32) for r in halves]
+        for r, v in zip(halves, pre):
+            a, d = gelu_pair(v)
+            act[r, :] = a.astype(BF)
+            slope[r, :] = d
+
+    def forward_out(j):
+        back = [jnp.dot(C[r, :], W[j, :, HB:], preferred_element_type=F32) for r in halves]
+        for r, v in zip(halves, back):
+            dpre[r, :] = (v * slope[r, :]).astype(BF)
 
     def product(r, k):
         q = slice(k * 256, k * 256 + 256)
@@ -207,7 +221,6 @@
     late_t = pl.ds(td, td)
 
     def tokens_own():
-        arrive(g1, 0, 2)
         for k, b in enumerate((T, C)):
             pltpu.make_async_copy(b.at[half_t], b.at[half_t], loc.at[1 + k]).wait()
 
@@ -219,10 +232,10 @@
 
     def rs(u, i):
         to = right if i in (0, 2, 4) else left
-        return send(sb.at[u, i], rb.at[u, i], rss.at[u, i], rsr.at[u, i], to)
+        return send(sb.at[u, i], rb.at[u, i], rss.at[0], rsr.at[u, min(i, 2)], to)
 
     def yc(u, i):
-        return send(ys.at[u, i], yr.at[u, i], ycs.at[u, i], ycr.at[u, i], across[i])
+        return send(ys.at[u, i], yr.at[u, i], ycs.at[0], ycr.at[u], across[i])
 
     def gx(u):
         return pool.at[u * 256 : (u + 1) * 256]
@@ -231,7 +244,7 @@
         at = NU * 256 + u * 256 + i * 128
         return pool.at[at : at + 128]
 
-    def grad(u):
+    def grad(u, ready=lambda: None, sent=lambda: None):
         a, b = ((T, dpre), (C, act))[u % 2]
         dims = (((0,), (0,)), ((), ()))
         far = lax.dot_general(a[:, 512:], b[...], dims, preferred_element_type=F32)
@@ -241,8 +254,15 @@
         gx(u)[...] = near[:256]
         gp(u, 0)[...] = near[256:384]
         gp(u, 1)[...] = far[384:]
-        for i in range(4):
+        ready()
+        for i in range(2):
             rs(u, i).start()
+        sent()
+        for i in range(2, 4):
+            rs(u, i).start()
+
+    def whole(ref, sem):
+        pltpu.make_async_copy(ref, ref, sem).wait()
 
     def reduce_one(u):
         for i in range(2):
@@ -251,8 +271,7 @@
             rs(u, 4 + i).start()
 
     def reduce_two(u):
-        for i in (2, 3, 4, 5):
-            rs(u, i).wait_recv()
+        whole(rb.at[u, pl.ds(2, 4)], rsr.at[u, 2])
         for r, a, b in ((upper, 3, 4), (lower, 2, 5)):
             gx(u)[r] = gx(u)[r] + rb[u, a].astype(F32) + rb[u, b].astype(F32)
         for i, (yy, cc) in enumerate(((1 - y, c), (1 - y, 1 - c), (y, 1 - c))):
@@ -267,20 +286,19 @@
         j, k = u // 2, u % 2
         return pl.ds(pl.multiple_of(k * 2048 + h * 1024 + j * HB, HB), HB)
 
-    def eight(i):
-        return pl.ds(pl.multiple_of(i * 8, 8), 8)
+    def piece(i):
+        return slice(i % 2 * 32, i % 2 * 32 + 32), slice(i // 2 * 128, i // 2 * 128 + 128)
 
     def send_delta(u, o):
         i = lax.rem(me + o, n)
-        return send(dl.at[u, eight(i)], dr.at[u, eight(me)], m1s.at[u], m1r.at[u], (i, s))
+        return send(dl.at[u, i], dr.at[u, me], m1s.at[0], m1r.at[u], (i, s))
 
     def send_mean(u, o):
         i = lax.rem(me + o, n)
-        return send(mr.at[u, eight(me)], mr.at[u, eight(me)], m2s.at[u], m2r.at[u], (i, s))
+        return send(mr.at[u, me], mr.at[u, me], m2s.at[0], m2r.at[u], (i, s))
 
     def step(u):
-        for i in range(3):
-            yc(u, i).wait_recv()
+        whole(yr.at[u], ycr.at[u])
         r = pl.ds(pl.multiple_of(y * 128 + c * 64, 64), 64)
         sums = (
             (c, gx(u)[r] + yr[u, 0].astype(F32)),
@@ -298,37 +316,41 @@
             b2[:, cols] = second
             out_copy(b1, o1, 0, cols).start()
             out_copy(b2, o2, 1, cols).start()
-            dl[u, :, pl.ds(pl.multiple_of(h * HB, HB), HB)] = ba[:, cols] - inner
+            delta = (ba[:, cols] - inner).astype(BF)
+            for i in range(4):
+                dl[u, 4 * h + i] = delta[piece(i)]
         for o in range(1, 8):
             send_delta(u, o).start()
 
-    def seven(ref, u, sem):
-        part_ = ref.at[u, pl.ds(0, 56)]
-        return pltpu.make_async_copy(part_, part_, sem)
-
     def mean(u):
-        seven(dr, u, m1r.at[u]).wait()
-        total = dl[u, eight(me)]
+        whole(dr.at[u, pl.ds(0, 7)], m1r.at[u])
+        total = dl[u, me].astype(F32)
         for o in range(1, 8):
-            total = total + dr[u, eight(lax.rem(me + o, n))]
-        mr[u, eight(me)] = total / n
+            total = total + dr[u, lax.rem(me + o, n)].astype(F32)
+        mr[u, me] = total / n
         for o in range(1, 8):
             send_mean(u, o).start()
 
     def outer(u):
-        seven(mr, u, m2r.at[u]).wait()
+        whole(mr.at[u, pl.ds(0, 7)], m2r.at[u])
         for h in range(2):
             cols = columns(u, h)
-            m = mr[u, :, h * HB : (h + 1) * HB]
-            momentum = 0.9 * bo[:, cols] + m
-            bo[:, cols] = momentum
-            ba[:, cols] = ba[:, cols] - 0.7 * (m + 0.9 * momentum)
+            start = u % 2 * 2048 + h * 1024 + u // 2 * HB
+            for i in range(4):
+                r, q_ = piece(i)
+                q_ = slice(start + q_.start, start + q_.stop)
+                m = mr[u, 4 * h + i]
+                momentum = 0.9 * bo[r, q_] + m
+                bo[r, q_] = momentum
+                ba[r, q_] = ba[r, q_] - 0.7 * (m + 0.9 * momentum)
             out_copy(bo, om, 2, cols).start()
             out_copy(ba, oa, 3, cols).start()
 
     pass_other(0)
     pass_own(0)
     pass_own(1)
+    pass_along_y(1)
+    near_y(2)
     pass_far(0)
     near_x(2)
     tokens_own()
@@ -339,78 +361,95 @@
     near_x(3)
     gather_end(0)
     lax.fori_loop(0, 2 * half, late, 0)
-    pass_own(2)
-
-    def both(f, j):
-        if 0 <= j < NJ:
-            f(2 * j + 1)
-            f(2 * j)
-
-    for j in range(NJ):
-        if j > 0:
-            gather_end(j)
-            forward(0, j)
-            if j == 2:
-                for cp in loads[1:]:
-                    cp.wait()
-            both(reduce_two, j - 2)
-            forward(1, j)
-            if j == 1:
-                pass_far(3)
-            both(reduce_one, j - 1)
-            both(mean, j - 3)
+
+    def second():
+        pass_own(2)
+        pass_along_y(2)
+
+    grad(1, ready=second)
+
+    def third():
+        pass_far(2)
+        near_y(3)
+        pass_own(3)
+        pass_along_y(3)
+
+    grad(0, ready=third)
+
+    def at(f, j, k):
+        if j >= 0:
+            f(2 * j + k)
+
+    p, q = NU - 2, NU - 1
+    for j in range(1, NJ):
+        gather_end(j)
+        forward_in(j)
+        at(reduce_one, j - 1, 1)
+        at(reduce_two, j - 2, 0)
+        at(mean, j - 3, 1)
+        at(step, j - 3, 0)
         grad(2 * j + 1)
-        if j == 0:
-            pass_own(3)
-        grad(2 * j)
-        if j == 0:
-            pass_far(2)
-        both(step, j - 2)
-        both(outer, j - 3)
-
-    p, q = NU - 2, NU - 1
-    both(reduce_two, NJ - 2)
-    reduce_one(q)
+        if j == 1:
+            pass_far(3)
+        forward_out(j)
+        if j == 2:
+            for cp in loads[1:]:
+                cp.wait()
+        at(reduce_one, j - 1, 0)
+        if j == NJ - 1:
+            at(step, j - 2, 1)
+        if j < NJ - 1:
+            grad(2 * j)
+        else:
+            grad(2 * j, sent=lambda: reduce_one(q))
+        at(reduce_two, j - 1, 1)
+        if j < NJ - 1:
+            at(step, j - 2, 1)
+        else:
+            at(mean, j - 3, 0)
+            at(step, j - 2, 0)
+        at(outer, j - 3, 1)
+
     reduce_one(p)
-    both(mean, NJ - 3)
-    both(step, NJ - 2)
+    at(outer, NJ - 4, 0)
+    reduce_two(p - 2)
+    mean(q - 4)
     reduce_two(q)
+    step(q - 2)
+    mean(p - 4)
     reduce_two(p)
-    both(outer, NJ - 3)
-    both(mean, NJ - 2)
+    step(p - 2)
     step(q)
+    mean(q - 2)
     step(p)
-    both(outer, NJ - 2)
+    outer(q - 4)
+    outer(p - 4)
+    mean(p - 2)
     mean(q)
     mean(p)
+    outer(q - 2)
+    outer(p - 2)
     outer(q)
     outer(p)
 
-    def drain(j, _):
-        for k in range(7):
-            g1(j, k).wait_send()
-        for k in (2, 3):
-            g2(j, k).wait_send()
-        return 0
-
-    def drain_sums(u, _):
-        for i in range(3):
-            yc(u, i).wait_send()
-        for i in range(6):
-            rs(u, i).wait_send()
-        seven(dl, u, m1s.at[u]).wait()
-        seven(mr, u, m2s.at[u]).wait()
-        return 0
-
-    lax.fori_loop(0, NJ, drain, 0)
-    for j in range(NJ):
-        for k in (6, 7, 8) if j else (0, 1, 4, 5):
-            g2(j, k).wait_send()
-    lax.fori_loop(0, NU, drain_sums, 0)
+    whole(W.at[:, pl.ds(0, 7 * 64)], s1s.at[0])
+    whole(W.at[:, pl.ds(0, 512)], s2s.at[0])
+    whole(sb, rss.at[0])
+    whole(ys, ycs.at[0])
+    whole(dl.at[pl.ds(0, NU - 1)], m1s.at[0])
+    whole(mr.at[pl.ds(0, NU - 1)], m2s.at[0])
     for k, b in enumerate((T, C)):
         pltpu.make_async_copy(b.at[half_t], b.at[half_t], tks.at[k]).wait()
     for k, (buf, ref) in enumerate(((b1, o1), (b2, o2), (bo, om), (ba, oa))):
         pltpu.make_async_copy(buf, ref, outs.at[k]).wait()
+
+
+def write(a, b, c, d, o1, o2, o3, o4, sems):
+    pairs = ((a, o1), (b, o2), (c, o3), (d, o4))
+    for wait in (False, True):
+        for i, (src, dst) in enumerate(pairs):
+            copy = pltpu.make_async_copy(src, dst, sems.at[i])
+            copy.wait() if wait else copy.start()
 
 
 def shards(tokens, cotangent, master, moment_one, moment_two, anchor, outer_momentum):
@@ -419,7 +458,7 @@
     vm = pltpu.VMEM
     dma = pltpu.SemaphoreType.DMA
     wide = jax.ShapeDtypeStruct((r, w), F32)
-    return pl.pallas_call(
+    results = pl.pallas_call(
         kernel,
         out_shape=(wide,) * 4,
         in_specs=[pl.BlockSpec(memory_space=pltpu.HBM)] * 7,
@@ -427,14 +466,14 @@
         scratch_shapes=[
             vm((2 * td, d), BF), vm((2 * td, d), BF), vm((NJ, d, 2 * HB), BF), vm((NJ, r, 2 * HB), BF),
             vm((r, w), F32), vm((r, w), F32), vm((r, w), F32), vm((r, w), F32), vm((r, w), F32),
-            vm((2 * td, HB), BF), vm((2 * td, HB), BF), vm((4 * td, HB), F32),
+            vm((2 * td, HB), BF), vm((2 * td, HB), BF), vm((2 * td, HB), F32), vm((4 * td, HB), F32),
             vm((NU, 6, 128, HB), BF), vm((NU, 6, 128, HB), BF),
             vm((NU, 3, r, HB), BF), vm((NU, 3, r, HB), BF),
-            vm((NU, r, 2 * HB), F32), vm((NU, r, 2 * HB), F32), vm((NU, r, 2 * HB), F32),
+            vm((NU, 8, 32, 128), BF), vm((NU, 8, 32, 128), BF), vm((NU, 8, 32, 128), F32),
             dma((7,)), dma((2,)), dma((2,)),
-            dma((NJ, 7)), dma((NJ, 7)), dma((NJ, 9)), dma((NJ, 9)),
-            dma((NU, 6)), dma((NU, 6)), dma((NU, 3)), dma((NU, 3)),
-            dma((NU,)), dma((NU,)), dma((NU,)), dma((NU,)), dma((4,)),
+            dma((1,)), dma((NJ, 3)), dma((1,)), dma((NJ, 3)),
+            dma((1,)), dma((NU, 3)), dma((1,)), dma((NU,)),
+            dma((1,)), dma((NU,)), dma((1,)), dma((NU,)), dma((4,)),
         ],
         compiler_params=pltpu.CompilerParams(
             collective_id=0, has_side_effects=True, vmem_limit_bytes=VMEM_MIB * 1024 * 1024
@@ -444,6 +483,15 @@
         ),
         name="outer_step",
     )(tokens, cotangent, master, moment_one, moment_two, anchor, outer_momentum)
+    return pl.pallas_call(
+        write,
+        out_shape=(wide,) * 4,
+        in_specs=[pl.BlockSpec(memory_space=pl.ANY)] * 4,
+        out_specs=(pl.BlockSpec(memory_space=pltpu.HBM),) * 4,
+        scratch_shapes=[dma((4,))],
+        compiler_params=pltpu.CompilerParams(vmem_limit_bytes=1024 * 1024),
+        name="write_results",
+    )(*results)
 
 
 def solution(mesh):

time: 97 us -> 89.6 us (0.924)
  local copies, waits for them, and re-layouts: 3.88 us -> 0 us
  Pallas kernels: 92.4 us -> 88.7 us
    pallas_call x1, Pallas kernels: 92.4 us -> 86.6 us  [shards(): pl.pallas_call(kernel, out_shape=(wide,) * 4, in_specs=[pl.BlockSpec(memo...]
    unnamed x4 -> x0, local copies, waits for them, and re-layouts: 3.88 us -> none
    pallas_call x0 -> x1, Pallas kernels: none -> 2.04 us  [shards(): pl.pallas_call(write, out_shape=(wide,) * 4, in_specs=[pl.BlockSpec(memor...]
where the time goes in v3:
time: 89.6 us; the launch traced here: 89.5 us
  Pallas kernels  88.7 us (99%)
    pallas_call x1, Pallas kernels, shards(): pl.pallas_call(kernel, out_shape=(wide,) * 4, in_specs=[pl.BlockSpec(memo...  86.6 us
    pallas_call x1, Pallas kernels, shards(): pl.pallas_call(write, out_shape=(wide,) * 4, in_specs=[pl.BlockSpec(memor...  2.04 us

profile of v3, /device:TPU:0, one launch (start us, length us, event | category | flops | bytes accessed | tf_op | source)
XLA Modules:
  0.0 89.5 jit_solution(6383822468891816487)
XLA Ops:
  0.6 86.6 %outer_step.1 = (f32[64,4096]{1,0:T(8,128)S(1)}, f32[64,4096]{1,0:T(8,128)S(1)}, f32[64,4096]{1,0:T(8,128)S(1)}, f32[64,4096]{1,0:T(8,128)S(1)}) custom-call(bf16[1536,1024]{1,0:T(8,128)(2,1)} %tok.1, bf16[1536,1024]{1,0:T(8,128)(2,1)} %cot.1, f32[64,4096]{1,0:T(8,128)} %mas.1, f32[64,4096]{1,0:T(8,128)} %mo1.1, f32[64,4096]{1,0:T(8,128)} %mo2.1, ...), custom_call_target="tpu_custom_call" | custom-call | flops 25769803776 | bytes 16777216 | tf_op jit(solution)/shard_map/outer_step/pallas_call | solution.py:461
  87.3 2.0 %write_results.1 = (f32[64,4096]{1,0:T(8,128)}, f32[64,4096]{1,0:T(8,128)}, f32[64,4096]{1,0:T(8,128)}, f32[64,4096]{1,0:T(8,128)}) custom-call(f32[64,4096]{1,0:T(8,128)S(1)} %get-tuple-element.8.a, f32[64,4096]{1,0:T(8,128)S(1)} %get-tuple-element.9.b, f32[64,4096]{1,0:T(8,128)S(1)} %get-tuple-element.10.c, f32[64,4096]{1,0:T(8,128)S(1)} %get-tuple-element.11.d), custom_call_target="tpu_custom_call" | custom-call | tf_op jit(solution)/shard_map/write_results/pallas_call | solution.py:486

commit v4 on v3

--- a/solution.py
+++ b/solution.py
@@ -159,6 +159,7 @@
     near_x(0)
     near_y(1)
     near_x(1)
+    near_y(2)
     for k, (a, b) in enumerate(((tok, T), (cot, C))):
         for cs, cd in blocks():
             send(a.at[:, cs], b.at[pl.ds(td, td), cd], tks.at[k], tkr.at[k], across[2]).start()
@@ -173,13 +174,13 @@
         act[r, :] = a.astype(BF)
         dpre[r, :] = (back * d).astype(BF)
 
+    halves = (slice(0, td), slice(td, 2 * td))
+
     def forward(i, j):
-        r = slice(i * td, (i + 1) * td)
+        r = halves[i]
         pre = jnp.dot(T[r, :], W[j, :, :HB], preferred_element_type=F32)
         back = jnp.dot(C[r, :], W[j, :, HB:], preferred_element_type=F32)
         finish(r, pre, back)
-
-    halves = (slice(0, td), slice(td, 2 * td))
 
     def forward_in(j):
         pre = [jnp.dot(T[r, :], W[j, :, :HB], preferred_element_type=F32) for r in halves]
@@ -350,7 +351,6 @@
     pass_own(0)
     pass_own(1)
     pass_along_y(1)
-    near_y(2)
     pass_far(0)
     near_x(2)
     tokens_own()
@@ -358,6 +358,7 @@
     tokens_other()
     lax.fori_loop(half, 2 * half, early, 0)
     pass_far(1)
+    near_y(3)
     near_x(3)
     gather_end(0)
     lax.fori_loop(0, 2 * half, late, 0)
@@ -367,14 +368,7 @@
         pass_along_y(2)
 
     grad(1, ready=second)
-
-    def third():
-        pass_far(2)
-        near_y(3)
-        pass_own(3)
-        pass_along_y(3)
-
-    grad(0, ready=third)
+    grad(0, ready=lambda: pass_own(3))
 
     def at(f, j, k):
         if j >= 0:
@@ -382,49 +376,55 @@
 
     p, q = NU - 2, NU - 1
     for j in range(1, NJ):
+        last = j == NJ - 1
         gather_end(j)
-        forward_in(j)
+        if j == 1:
+            forward(0, j)
+            pass_far(2)
+            pass_along_y(3)
+            forward(1, j)
+        else:
+            forward_in(j)
         at(reduce_one, j - 1, 1)
         at(reduce_two, j - 2, 0)
-        at(mean, j - 3, 1)
-        at(step, j - 3, 0)
+        if last:
+            step(1)
+            step(0)
         grad(2 * j + 1)
         if j == 1:
             pass_far(3)
-        forward_out(j)
+        else:
+            forward_out(j)
         if j == 2:
             for cp in loads[1:]:
                 cp.wait()
         at(reduce_one, j - 1, 0)
-        if j == NJ - 1:
-            at(step, j - 2, 1)
-        if j < NJ - 1:
+        if last:
+            step(3)
+            grad(2 * j, sent=lambda: reduce_one(q))
+        else:
             grad(2 * j)
-        else:
-            grad(2 * j, sent=lambda: reduce_one(q))
         at(reduce_two, j - 1, 1)
-        if j < NJ - 1:
-            at(step, j - 2, 1)
-        else:
-            at(mean, j - 3, 0)
-            at(step, j - 2, 0)
-        at(outer, j - 3, 1)
-
+
+    step(2)
+    mean(1)
+    mean(0)
     reduce_one(p)
-    at(outer, NJ - 4, 0)
     reduce_two(p - 2)
-    mean(q - 4)
     reduce_two(q)
+    mean(3)
+    reduce_two(p)
+    mean(2)
     step(q - 2)
-    mean(p - 4)
-    reduce_two(p)
     step(p - 2)
     step(q)
+    outer(1)
+    outer(0)
+    step(p)
     mean(q - 2)
-    step(p)
-    outer(q - 4)
-    outer(p - 4)
     mean(p - 2)
+    outer(3)
+    outer(2)
     mean(q)
     mean(p)
     outer(q - 2)

time: 89.6 us -> 87.4 us (0.975)
  Pallas kernels: 88.7 us -> 85.8 us
    pallas_call x1, Pallas kernels: 86.6 us -> 83.8 us  [shards(): pl.pallas_call(kernel, out_shape=(wide,) * 4, in_specs=[pl.BlockSpec(memo...]
where the time goes in v4:
time: 87.4 us; the launch traced here: 86.6 us
  Pallas kernels  85.8 us (98%)
    pallas_call x1, Pallas kernels, shards(): pl.pallas_call(kernel, out_shape=(wide,) * 4, in_specs=[pl.BlockSpec(memo...  83.8 us
    pallas_call x1, Pallas kernels, shards(): pl.pallas_call(write, out_shape=(wide,) * 4, in_specs=[pl.BlockSpec(memor...  2.04 us

profile of v4, /device:TPU:0, one launch (start us, length us, event | category | flops | bytes accessed | tf_op | source)
XLA Modules:
  0.0 86.6 jit_solution(3261875761028723169)
XLA Ops:
  0.6 83.8 %outer_step.1 = (f32[64,4096]{1,0:T(8,128)S(1)}, f32[64,4096]{1,0:T(8,128)S(1)}, f32[64,4096]{1,0:T(8,128)S(1)}, f32[64,4096]{1,0:T(8,128)S(1)}) custom-call(bf16[1536,1024]{1,0:T(8,128)(2,1)} %tok.1, bf16[1536,1024]{1,0:T(8,128)(2,1)} %cot.1, f32[64,4096]{1,0:T(8,128)} %mas.1, f32[64,4096]{1,0:T(8,128)} %mo1.1, f32[64,4096]{1,0:T(8,128)} %mo2.1, ...), custom_call_target="tpu_custom_call" | custom-call | flops 25769803776 | bytes 16777216 | tf_op jit(solution)/shard_map/outer_step/pallas_call | solution.py:461
  84.4 2.0 %write_results.1 = (f32[64,4096]{1,0:T(8,128)}, f32[64,4096]{1,0:T(8,128)}, f32[64,4096]{1,0:T(8,128)}, f32[64,4096]{1,0:T(8,128)}) custom-call(f32[64,4096]{1,0:T(8,128)S(1)} %get-tuple-element.8.a, f32[64,4096]{1,0:T(8,128)S(1)} %get-tuple-element.9.b, f32[64,4096]{1,0:T(8,128)S(1)} %get-tuple-element.10.c, f32[64,4096]{1,0:T(8,128)S(1)} %get-tuple-element.11.d), custom_call_target="tpu_custom_call" | custom-call | tf_op jit(solution)/shard_map/write_results/pallas_call | solution.py:486
